TPU v7x, 8 devices: a whole 2x2x1 slice. The times are simulated.
8 devices in a mesh: data: 1 (over z), seq: 2 (over y), dap: 4 (over x, core).
Axes of the slice: x: 2, y: 2, z: 1, core: 2. Of those that a mesh axis runs over, the one named last changes fastest.
Arguments:
- msa_act: bfloat16 [256, 384, 64], P(('data', 'seq', 'dap'))
- msa_mask: int32 [256, 384], P(('data', 'seq', 'dap'))
- pair_act: float32 [384, 384, 128], P(('data', 'dap'))
- ln_gamma: bfloat16 [64], replicated
- ln_beta: bfloat16 [64], replicated
- w_a: bfloat16 [64, 32], replicated
- b_a: bfloat16 [32], replicated
- w_b: bfloat16 [64, 32], replicated
- b_b: bfloat16 [32], replicated
- w_out: bfloat16 [1024, 128], replicated
- b_out: bfloat16 [128], replicated
Outputs:
- output: float32 [384, 384, 128], P(('data', 'dap'))
All inputs are finite; a program needn't handle non-finite values.
Results may differ from a plain program's by a relative error of at most 0.00769173.
Values are sent between devices in bfloat16 or wider.
A program may use at most 1 GiB of HBM per device.

v0:
```python
import jax
import jax.numpy as jnp
from jax import lax
from jax.sharding import PartitionSpec as P


def layer_norm(value_a7, ln_gamma, ln_beta):
    values = value_a7.astype(jnp.float32)
    row_mean = jnp.mean(values, axis=-1, keepdims=True)
    centered = values - row_mean
    variance = jnp.mean(centered * centered, axis=-1, keepdims=True)
    normed = centered * lax.rsqrt(variance + 1e-5)
    return (normed * ln_gamma.astype(jnp.float32) + ln_beta.astype(jnp.float32)).astype(jnp.bfloat16)


def project(normed, weight, bias_vec, seq_keep):
    summed = jnp.einsum('...k,kc->...c', normed, weight, preferred_element_type=jnp.float32)
    return ((summed + bias_vec.astype(jnp.float32)) * seq_keep[..., None]).astype(jnp.bfloat16)


def solution(mesh):
    value_a8 = P(('data', 'seq', 'dap'), None, None)
    mask_spec = P(('data', 'seq', 'dap'), None)
    pair_spec = P(('data', 'dap'), None, None)

    def device_step(value_a9, mask_local, pair_local, ln_gamma, ln_beta, w_a, b_a, w_b, b_b, w_out, b_out):
        hidden = w_a.shape[1]
        pair_dim = w_out.shape[1]
        normed = layer_norm(value_a9, ln_gamma, ln_beta)
        seq_keep = mask_local.astype(jnp.bfloat16)
        left = project(normed, w_a, b_a, seq_keep)
        right = project(normed, w_b, b_b, seq_keep)
        w_cube = w_out.reshape(hidden, hidden, pair_dim)
        lifted = jnp.einsum('sic,cde->side', left, w_cube, preferred_element_type=jnp.float32).astype(jnp.bfloat16)
        part_r = jnp.einsum('side,sjd->ije', lifted, right, preferred_element_type=jnp.float32).astype(jnp.bfloat16)
        part_n = jnp.einsum('si,sj->ij', seq_keep, seq_keep, preferred_element_type=jnp.float32)
        rows_r = lax.psum_scatter(part_r, 'dap', scatter_dimension=0, tiled=True)
        rows_n = lax.psum_scatter(part_n, 'dap', scatter_dimension=0, tiled=True)
        rows_r = lax.psum(rows_r, 'seq')
        rows_n = lax.psum(rows_n, 'seq')
        update = (rows_r.astype(jnp.float32) + b_out.astype(jnp.float32)) / (1e-3 + rows_n[..., None])
        return pair_local + update

    return jax.shard_map(device_step, mesh=mesh, in_specs=(value_a8, mask_spec, pair_spec, P(), P(), P(), P(), P(), P(), P(), P()), out_specs=pair_spec, check_vma=False)
```

profile of v0, /device:TPU:0, one launch (start us, length us, event | category | flops | bytes accessed | tf_op | source)
XLA Modules:
  0.0 608.3 jit_solution(340898436317497802)
XLA Ops:
  6.5 0.0 copy-start
  6.5 0.0 copy-start.2
  6.5 0.0 copy-start.5
  6.5 0.0 copy-start.6
  6.5 0.0 copy-start.7
  6.5 0.0 reduce-scatter.5.cloned.1.call-start
  6.6 2.1 fusion.24
  8.7 0.0 reduce-scatter.5.cloned.1.call-update
  8.7 0.0 reduce-scatter.3.cloned.1.call-start
  8.7 0.8 convert_convert_fusion
  9.5 0.0 copy-start.3
  9.5 1.7 convert_reduce_fusion
  11.3 0.0 copy-done.2
  11.3 0.6 fusion.9
  11.9 0.0 copy-done.5
  11.9 0.0 copy-done.6
  11.9 0.0 copy-done.7
  11.9 0.7 fusion.12
  12.7 0.0 copy-done.3
  12.7 0.4 fusion.26
  13.1 0.0 copy-start.4
  13.1 1.0 fusion.19
  14.0 0.0 copy-start.8
  14.0 5.5 copy.14
  19.6 0.0 copy-done.4
  19.6 0.4 fusion.28
  20.0 0.0 copy-done.8
  20.0 1.0 fusion.45
  20.9 0.0 copy-done
  20.9 71.0 %fusion.4 = bf16[384,384,128]{2,1,0:T(8,128)(2,1)} fusion(bf16[32,384,32,1]{2,0,3,1:T(8,128)(2,1)} %copy.14, bf16[32,32,128,1]{2,1,0,3:T(8,128)(2,1)S(1)} %bitcast.36, bf16[32,384,32,1]{1,0,2,3:T(8,128)(2,1)S(1)} %fusion.45), kind=kOutput, calls=%fused_computation.4 | convolution fusion | flops 41945137152 | bytes 39583744 | tf_op jit(solution)/shard_map/side,sjd->ije/dot_general | solution.py:35
  91.9 0.0 reduce-scatter.3.cloned.1.call-update
  91.9 0.0 all-reduce.5.cloned.1.call-start
  92.0 0.0 reduce-scatter.5.cloned.1.call-done
  92.0 0.7 all-reduce.5.cloned.1.call-update
  92.7 0.0 all-reduce.3.cloned.1.call-start
  92.7 253.4 %reduce-scatter.3.cloned.1.call-done = bf16[96,384,128]{2,1,0:T(8,128)(2,1)} async-done(((bf16[384,384,128]{2,1,0:T(8,128)(2,1)}), bf16[96,384,128]{2,1,0:T(8,128)(2,1)}) %reduce-scatter.3.cloned.1.call-update) | async-done | bytes 9437200 | tf_op jit(solution)/shard_map/reduce_scatter | solution.py:37
  346.1 0.0 copy-start.9
  346.1 0.0 all-reduce.3.cloned.1.call-update
  346.2 0.6 copy-done.9
  346.8 17.6 %all-reduce.5.cloned.1.call-done = f32[96,384]{1,0:T(8,128)} async-done(((f32[96,384]{1,0:T(8,128)}), f32[96,384]{1,0:T(8,128)}) %all-reduce.5.cloned.1.call-update) | async-done | bytes 147472 | tf_op jit(solution)/shard_map/psum | solution.py:40
  364.4 0.9 broadcast_add_fusion
  365.4 216.2 %all-reduce.3.cloned.1.call-done = bf16[96,384,128]{2,1,0:T(8,128)(2,1)} async-done(((bf16[96,384,128]{2,1,0:T(8,128)(2,1)}), bf16[96,384,128]{2,1,0:T(8,128)(2,1)}) %all-reduce.3.cloned.1.call-update) | async-done | bytes 9437200 | tf_op jit(solution)/shard_map/psum | solution.py:39
  581.5 0.0 copy-start.1
  581.5 20.2 %divide_add_fusion = f32[96,384,128]{2,1,0:T(8,128)} fusion(f32[96,384,128]{2,1,0:T(8,128)} %param.13, bf16[96,384,128]{2,1,0:T(8,128)(2,1)} %all-reduce.3.cloned.1.call-done, f32[96,384]{1,0:T(8,128)S(1)} %broadcast_add_fusion, f32[128]{0:T(128)S(1)} %convert_element_type.61), kind=kLoop, calls=%fused_computation.5 | loop fusion | flops 18874368 | bytes 47333888 | tf_op jit(solution)/shard_map/add | solution.py:42
  601.7 0.0 copy-done.1
  (7 shorter events, 0.0 us)
Async XLA Ops:
  6.5 14.4 %copy-start = (bf16[1024,128]{1,0:T(8,128)(2,1)S(1)}, bf16[1024,128]{1,0:T(8,128)(2,1)}, u32[]{:S(2)}) copy-start(bf16[1024,128]{1,0:T(8,128)(2,1)} %param.20) | copy-start | bytes 786436
  6.5 4.7 copy-start.2
  6.5 5.3 copy-start.5
  6.5 5.4 copy-start.6
  6.5 5.4 copy-start.7
  6.5 85.5 %reduce-scatter.5.cloned.1.call-start = ((), (), s32[]{:S(2)}) async-start(), calls=%async_computation.4 | async-start | bytes 737280 | tf_op jit(solution)/shard_map/reduce_scatter | solution.py:38
  8.7 337.5 %reduce-scatter.3.cloned.1.call-start = ((), (), s32[]{:S(2)}) async-start(), calls=%async_computation.2 | async-start | bytes 47185920 | tf_op jit(solution)/shard_map/reduce_scatter | solution.py:37
  9.5 3.1 copy-start.3
  13.1 6.5 %copy-start.4 = (bf16[64,32]{0,1:T(8,128)(2,1)S(1)}, bf16[64,32]{0,1:T(8,128)(2,1)}, u32[]{:S(2)}) copy-start(bf16[64,32]{0,1:T(8,128)(2,1)} %param.18) | copy-start | bytes 12292
  14.0 5.9 copy-start.8
  91.9 272.5 %all-reduce.5.cloned.1.call-start = ((), (), s32[]{:S(2)}) async-start(), calls=%async_computation.5 | async-start | bytes 294912 | tf_op jit(solution)/shard_map/psum | solution.py:40
  92.7 488.9 %all-reduce.3.cloned.1.call-start = ((), (), s32[]{:S(2)}) async-start(), calls=%async_computation.3 | async-start | bytes 18874368 | tf_op jit(solution)/shard_map/psum | solution.py:39
  346.1 0.7 copy-start.9
  581.5 20.2 %copy-start.1 = (bf16[1024,128]{1,0:T(8,128)(2,1)S(1)}, bf16[1024,128]{1,0:T(8,128)(2,1)}, u32[]{:S(2)}) copy-start(bf16[1024,128]{1,0:T(8,128)(2,1)} %param.20) | copy-start | bytes 786436
Sparse Core Ops, SparseCore 0:
  9.8 19.2 reduce-scatter.4
  92.1 254.0 reduce-scatter.2
  348.4 15.9 all-reduce.4
  366.7 214.7 all-reduce.2
where the time goes:
time: 609 us; the launch traced here: 608 us
  waiting for transfers between devices  488 us (80%)
  matrix products  73.7 us (12%)
  other arithmetic  26.9 us (4%)
  between operations  13.3 us (2%)
  local copies, waits for them, and re-layouts  6.22 us (1%)
    reduce_scatter x1, waiting for transfers between devices, device_step(): rows_r = lax.psum_scatter(part_r, 'dap', scatter_dimension=0, tiled=True)  253 us
    psum x1, waiting for transfers between devices, device_step(): rows_r = lax.psum(rows_r, 'seq')  216 us
    dot_general x1, matrix products, device_step(): jnp.einsum('side,sjd->ije', lifted, right, preferred_element_type=jnp.flo...  71 us
    add x1, other arithmetic, device_step(): return pair_local + update  20.2 us
    psum x1, waiting for transfers between devices, device_step(): rows_n = lax.psum(rows_n, 'seq')  17.6 us
  transfers between devices with their start and end apart: 4, of which 3 were waited for; matrix products, arithmetic and copies ran while one was open for 14% of the time, Pallas kernels for 0%

commit v1 on v0

v1 whole, which is shorter than its diff:
```python
import functools

import jax
import jax.numpy as jnp
from jax import lax
from jax.experimental import pallas as pl
from jax.experimental.pallas import tpu as pltpu
from jax.sharding import PartitionSpec as P

MESH = pl.DeviceIdType.MESH
S_LOC, N, K, C, E = 32, 384, 64, 32, 128
S = 256
ROWS = 96
JC = 3
CG = 8
D_VIA_X = 24
IB = 8


def exchange_kernel(x_ref, mask_ref, par_ref, wt_ref, wo_ref,
                    at_ref, ball_ref, inv_ref, wot_ref,
                    stage, ta, ra, rp, mall, atf, wof, ns, ssem, rsem):
    y = lax.axis_index('seq')
    r = lax.axis_index('dap')
    x = r // 2
    c = r % 2
    me = y * 4 + r
    dev_x = (0, y, (1 - x) * 2 + c)
    dev_y = (0, 1 - y, r)
    dev_p = (0, y, x * 2 + 1 - c)
    id_x = y * 4 + (1 - x) * 2 + c
    id_y = (1 - y) * 4 + r
    id_xy = (1 - y) * 4 + (1 - x) * 2 + c
    id_p = y * 4 + x * 2 + 1 - c

    barrier = pltpu.get_barrier_semaphore()
    flips = [(fy, fr) for fy in range(2) for fr in range(4) if fy or fr]
    for fy, fr in flips:
        peer = (0, (y + fy) % 2, (r + fr) % 4)
        pl.semaphore_signal(barrier, inc=1, device_id=peer, device_id_type=MESH)

    gamma, beta, bias = par_ref[:, 0:1], par_ref[:, 1:2], par_ref[:, 2:3]
    wt = wt_ref[...]

    def one_seq(s, carry):
        v = x_ref[s].astype(jnp.float32)
        mean = jnp.sum(v, axis=0, keepdims=True) * (1.0 / K)
        cen = v - mean
        var = jnp.sum(cen * cen, axis=0, keepdims=True) * (1.0 / K)
        xn = (cen * lax.rsqrt(var + 1e-5) * gamma + beta).astype(jnp.bfloat16)
        out = jnp.dot(wt, xn, preferred_element_type=jnp.float32)
        keep = mask_ref[pl.ds(s, 1), :].astype(jnp.float32)
        out = (out + bias) * keep
        for t in range(3):
            stage[t, pl.ds(s, 2 * C, stride=S_LOC), :] = out[:, t * 128:(t + 1) * 128]
        return carry

    lax.fori_loop(0, S_LOC, one_seq, 0, unroll=4)

    my_rows = pl.ds(pl.multiple_of(me * S_LOC, S_LOC), S_LOC)

    for g in range(CG):
        for t in range(3):
            blk = stage[t, g * 128:(g + 1) * 128, :]
            blk = blk.T.astype(jnp.bfloat16)
            lo = t * 128
            while lo < (t + 1) * 128:
                q = lo // ROWS
                hi = min((q + 1) * ROWS, (t + 1) * 128)
                ta[q, g, lo - q * ROWS:hi - q * ROWS, :] = blk[lo - t * 128:hi - t * 128, :]
                lo = hi
    for d in range(C):
        for t in range(JC):
            row = stage[t, (C + d) * S_LOC:(C + d + 1) * S_LOC, :]
            ball_ref[t, d, my_rows, :] = row.astype(jnp.bfloat16)
    mall[my_rows, :] = mask_ref[...].astype(jnp.float32).astype(jnp.bfloat16)

    pl.semaphore_wait(barrier, 7)

    sends = []

    def copy(src, dst, k, dev):
        return pltpu.make_async_remote_copy(
            src_ref=src, dst_ref=dst, send_sem=ssem.at[k], recv_sem=rsem.at[k],
            device_id=dev, device_id_type=MESH)

    def send(src, dst, k, dev):
        cp = copy(src, dst, k, dev)
        cp.start()
        sends.append(cp)

    def arrived(ref, k):
        copy(ref, ref, k, dev_p).wait_recv()

    def rows_of(dev_id):
        return pl.ds(pl.multiple_of(dev_id * S_LOC, S_LOC), S_LOC)

    def b_part(t, dev_id, lo=0, hi=C):
        return ball_ref.at[t, pl.ds(lo, hi - lo), rows_of(dev_id), :]

    A_X, A_Y, A_XY = 0, 1, 2
    A_P = {'o': 3, 'x': 4, 'y': 5, 'd': 6}
    M0 = 7

    def bk(t, what):
        return 14 + t * 9 + ['x', 'y', 'dx', 'dy', 'po', 'px', 'py', 'pdx', 'pdy'].index(what)

    own = 2 * x
    other = 2 * (1 - x)
    send(ta.at[pl.ds(other, 2)], ra.at[0], A_X, dev_x)
    send(ta.at[pl.ds(own, 2)], ra.at[1], A_Y, dev_y)
    send(ta.at[own + 1 - c], rp.at[0], A_P['o'], dev_p)
    for n, (fy, fr) in enumerate(flips):
        peer = (0, (y + fy) % 2, (r + fr) % 4)
        send(mall.at[my_rows], mall.at[my_rows], M0 + n, peer)

    def send_own(t, to):
        dev = {'x': dev_x, 'y': dev_y, 'po': dev_p}[to]
        send(b_part(t, me), b_part(t, me), bk(t, to), dev)

    send_own(0, 'x')
    send_own(0, 'po')

    wof[...] = wo_ref[...].astype(jnp.float32)
    for g in range(CG):
        parts = [wof[pl.ds(4 * g + k, C, stride=C), :] for k in range(4)]
        blk = jnp.concatenate(parts, axis=0)
        wot_ref[:, g * 128:(g + 1) * 128] = blk.T.astype(jnp.bfloat16)

    def got_b(t, frm):
        if frm == 'x':
            arrived(b_part(t, id_x), bk(t, 'x'))
            send(b_part(t, id_x, D_VIA_X, C), b_part(t, id_x, D_VIA_X, C), bk(t, 'dy'), dev_y)
            send(b_part(t, id_x), b_part(t, id_x), bk(t, 'px'), dev_p)
        elif frm == 'y':
            arrived(b_part(t, id_y), bk(t, 'y'))
            send(b_part(t, id_y, 0, D_VIA_X), b_part(t, id_y, 0, D_VIA_X), bk(t, 'dx'), dev_x)
            send(b_part(t, id_y), b_part(t, id_y), bk(t, 'py'), dev_p)
        elif frm == 'dx':
            ref = b_part(t, id_xy, 0, D_VIA_X)
            arrived(ref, bk(t, 'dx'))
            send(ref, ref, bk(t, 'pdx'), dev_p)
        else:
            ref = b_part(t, id_xy, D_VIA_X, C)
            arrived(ref, bk(t, 'dy'))
            send(ref, ref, bk(t, 'pdy'), dev_p)

    arrived(ra.at[0], A_X)
    send(ra.at[0], ra.at[2], A_XY, dev_y)
    send(ra.at[0, 1 - c], rp.at[1], A_P['x'], dev_p)
    send_own(0, 'y')
    send_own(1, 'x')
    arrived(ra.at[1], A_Y)
    send(ra.at[1, 1 - c], rp.at[2], A_P['y'], dev_p)
    got_b(0, 'x')
    send_own(1, 'y')
    send_own(1, 'po')
    send_own(2, 'x')
    arrived(ra.at[2], A_XY)
    send(ra.at[2, 1 - c], rp.at[3], A_P['d'], dev_p)
    got_b(0, 'y')
    send_own(2, 'y')
    send_own(2, 'po')
    for k, name in enumerate(['o', 'x', 'y', 'd']):
        arrived(rp.at[k], A_P[name])

    lane = lax.broadcasted_iota(jnp.int32, (ROWS, 128), 1)
    low = lane < 64
    odd = lax.rem(lane // 32, 2) == 1

    for half in range(2):
        for g in range(CG):
            v = []
            for q in range(4):
                sx, sc = q // 2, q % 2
                same_c = sc == c
                dx = (sx != x).astype(jnp.int32)
                dy = (half != y).astype(jnp.int32)
                slot = dx + 2 * dy
                own_v = ta[r, g].astype(jnp.float32)
                ra_slot = jnp.maximum(slot - 1, 0)
                in_plane = jnp.where(slot == 0, own_v, ra[ra_slot, c, g].astype(jnp.float32))
                v.append(jnp.where(same_c, in_plane, rp[slot, g].astype(jnp.float32)))
            r0, r1, r2, r3 = [pltpu.roll(u, 64, 1) for u in v]
            n0 = jnp.where(low, v[0], r2)
            n1 = jnp.where(low, v[1], r3)
            n2 = jnp.where(low, r0, v[2])
            n3 = jnp.where(low, r1, v[3])
            w0 = jnp.where(odd, pltpu.roll(n1, 32, 1), n0)
            w1 = jnp.where(odd, n1, pltpu.roll(n0, 96, 1))
            w2 = jnp.where(odd, pltpu.roll(n3, 32, 1), n2)
            w3 = jnp.where(odd, n3, pltpu.roll(n2, 96, 1))
            for k, w in enumerate((w0, w1, w2, w3)):
                atf[half, pl.ds(4 * g + k, ROWS, stride=C), :] = w
    for blk in range(12):
        for half in range(2):
            at_ref[blk * 256:(blk + 1) * 256, half * 128:(half + 1) * 128] = (
                atf[half, blk * 256:(blk + 1) * 256, :].astype(jnp.bfloat16))

    got_b(1, 'x')
    got_b(1, 'y')
    got_b(0, 'dx')
    got_b(0, 'dy')
    got_b(2, 'x')
    got_b(2, 'y')

    for n, (fy, fr) in enumerate(flips):
        frm = ((y - fy + 2) % 2) * 4 + (r - fr + 4) % 4
        arrived(mall.at[rows_of(frm)], M0 + n)
    m = mall[...]
    ns[...] = lax.dot_general(m, m, (((0,), (0,)), ((), ())), preferred_element_type=jnp.float32)
    inv_ref[...] = 1.0 / (1e-3 + ns[pl.ds(pl.multiple_of(r * ROWS, ROWS), ROWS), :])

    for t in (1, 2):
        got_b(t, 'dx')
        got_b(t, 'dy')
    id_px = y * 4 + (1 - x) * 2 + 1 - c
    id_py = (1 - y) * 4 + x * 2 + 1 - c
    id_pd = (1 - y) * 4 + (1 - x) * 2 + 1 - c
    for t in range(JC):
        arrived(b_part(t, id_p), bk(t, 'po'))
        arrived(b_part(t, id_px), bk(t, 'px'))
        arrived(b_part(t, id_py), bk(t, 'py'))
        arrived(b_part(t, id_pd, 0, D_VIA_X), bk(t, 'pdx'))
        arrived(b_part(t, id_pd, D_VIA_X, C), bk(t, 'pdy'))
    for cp in sends:
        cp.wait_send()


def exchange(xt, mask, par, wt, w_out):
    vm = pl.BlockSpec(memory_space=pltpu.VMEM)
    nsem = 14 + 9 * JC
    return pl.pallas_call(
        exchange_kernel,
        out_shape=(
            jax.ShapeDtypeStruct((ROWS * C, S), jnp.bfloat16),
            jax.ShapeDtypeStruct((JC, C, S, 128), jnp.bfloat16),
            jax.ShapeDtypeStruct((ROWS, N), jnp.float32),
            jax.ShapeDtypeStruct((E, C * C), jnp.bfloat16),
        ),
        in_specs=[vm] * 5,
        out_specs=(vm,) * 4,
        scratch_shapes=[
            pltpu.VMEM((3, 2 * C * S_LOC, 128), jnp.float32),
            pltpu.VMEM((4, CG, ROWS, 128), jnp.bfloat16),
            pltpu.VMEM((3, 2, CG, ROWS, 128), jnp.bfloat16),
            pltpu.VMEM((4, CG, ROWS, 128), jnp.bfloat16),
            pltpu.VMEM((S, N), jnp.bfloat16),
            pltpu.VMEM((2, ROWS * C, 128), jnp.float32),
            pltpu.VMEM((C * C, E), jnp.float32),
            pltpu.VMEM((N, N), jnp.float32),
            pltpu.SemaphoreType.DMA((nsem,)),
            pltpu.SemaphoreType.DMA((nsem,)),
        ],
        compiler_params=pltpu.CompilerParams(
            collective_id=0, has_side_effects=True, vmem_limit_bytes=60 * 1024 * 1024),
        name='exchange',
    )(xt, mask, par, wt, w_out)


def form_kernel(at_ref, ball_ref, inv_ref, wot_ref, bo_ref, z_ref, out_ref, hi_ref, lo_ref):
    at = at_ref[...]
    for p in range(C // 2):
        rhs = jnp.concatenate([ball_ref[0, 2 * p], ball_ref[0, 2 * p + 1]], axis=1)
        o = jnp.dot(at, rhs, preferred_element_type=jnp.float32)
        hi = o.astype(jnp.bfloat16)
        lo = (o - hi.astype(jnp.float32)).astype(jnp.bfloat16)
        for i in range(IB):
            for k in range(2):
                rr = slice((2 * p + k) * C, (2 * p + k + 1) * C)
                ll = slice(i * 128, (i + 1) * 128)
                hi_ref[rr, ll] = hi[i * C:(i + 1) * C, k * 128:(k + 1) * 128]
                lo_ref[rr, ll] = lo[i * C:(i + 1) * C, k * 128:(k + 1) * 128]
    wot = wot_ref[...]
    bo = bo_ref[...]
    for q in range(IB // 2):
        ll = slice(q * 256, (q + 1) * 256)
        rt = jnp.dot(wot, hi_ref[:, ll], preferred_element_type=jnp.float32)
        rt = rt + jnp.dot(wot, lo_ref[:, ll], preferred_element_type=jnp.float32)
        for k in range(2):
            i = 2 * q + k
            upd = (rt[:, k * 128:(k + 1) * 128] + bo) * inv_ref[i:i + 1, :]
            out_ref[i] = z_ref[i] + upd.T


def form(at, ball, inv, wot, bo, z):
    return pl.pallas_call(
        form_kernel,
        grid=(JC, ROWS // IB),
        out_shape=jax.ShapeDtypeStruct((ROWS, N, E), jnp.float32),
        in_specs=[
            pl.BlockSpec((IB * C, S), lambda j, i: (i, 0)),
            pl.BlockSpec((1, C, S, 128), lambda j, i: (j, 0, 0, 0)),
            pl.BlockSpec((IB, 128), lambda j, i: (i, j)),
            pl.BlockSpec((E, C * C), lambda j, i: (0, 0)),
            pl.BlockSpec((E, 1), lambda j, i: (0, 0)),
            pl.BlockSpec((IB, 128, E), lambda j, i: (i, j, 0)),
        ],
        out_specs=pl.BlockSpec((IB, 128, E), lambda j, i: (i, j, 0)),
        scratch_shapes=[
            pltpu.VMEM((C * C, IB * 128), jnp.bfloat16),
            pltpu.VMEM((C * C, IB * 128), jnp.bfloat16),
        ],
        compiler_params=pltpu.CompilerParams(vmem_limit_bytes=40 * 1024 * 1024),
        name='form',
    )(at, ball, inv, wot, bo, z)


def solution(mesh):
    rows = P(('data', 'seq', 'dap'), None, None)
    mask_spec = P(('data', 'seq', 'dap'), None)
    pair_spec = P(('data', 'dap'), None, None)

    def device_step(msa, mask, pair, ln_gamma, ln_beta, w_a, b_a, w_b, b_b, w_out, b_out):
        xt = jnp.swapaxes(msa, 1, 2)
        wt = jnp.concatenate([w_a.T, w_b.T], axis=0)
        par = jnp.stack([ln_gamma, ln_beta, jnp.concatenate([b_a, b_b])], axis=1).astype(jnp.float32)
        at, ball, inv, wot = exchange(xt, mask, par, wt, w_out)
        bo = b_out.astype(jnp.float32)[:, None]
        return form(at, ball, inv, wot, bo, pair)

    return jax.shard_map(device_step, mesh=mesh, in_specs=(rows, mask_spec, pair_spec) + (P(),) * 8,
                         out_specs=pair_spec, check_vma=False)
```

time: 609 us -> 133 us (0.22)
  waiting for transfers between devices: 488 us -> 0 us
  Pallas kernels: 0 us -> 122 us
  matrix products: 73.7 us -> 0 us
  other arithmetic: 26.9 us -> 3.4 us
  between operations: 13.3 us -> 0.02 us
    reduce_scatter x2 -> x0, waiting for transfers between devices: 253 us -> none  [the longest x1 253 us: device_step(): rows_r = lax.psum_scatter(part_r, 'dap', scatter_dimension=0, tiled=True)]
    psum x2 -> x0, waiting for transfers between devices: 234 us -> none  [the longest x1 216 us: device_step(): rows_r = lax.psum(rows_r, 'seq')]
    pallas_call x0 -> x2, Pallas kernels: none -> 122 us  [the longest x1 63 us: form(): pl.pallas_call(form_kernel, grid=(JC, ROWS // IB), out_shape=jax.ShapeDty...]
    dot_general x4 -> x0, matrix products: 73.7 us -> none  [the longest x1 71 us: device_step(): jnp.einsum('side,sjd->ije', lifted, right, preferred_element_type=jnp.flo...]
    add x2 -> x0, other arithmetic: 21.1 us -> none  [the longest x1 20.2 us: device_step(): return pair_local + update]
  transfers between devices with their start and end apart: 4 -> 0, of which waited for: 3 -> 0; matrix products, arithmetic and copies ran while one was open for 14% -> 0% of each run, Pallas kernels for 0% -> 0%
where the time goes in v1:
time: 133 us; the launch traced here: 132 us
  Pallas kernels  122 us (92%)
  local copies, waits for them, and re-layouts  6.86 us (5%)
  other arithmetic  3.4 us (3%)
    pallas_call x1, Pallas kernels, form(): pl.pallas_call(form_kernel, grid=(JC, ROWS // IB), out_shape=jax.ShapeDty...  63 us
    pallas_call x1, Pallas kernels, exchange(): pl.pallas_call(exchange_kernel, out_shape=(jax.ShapeDtypeStruct((ROWS * C...  59.1 us
    unnamed x8, local copies, waits for them, and re-layouts  6.04 us

profile of v1, /device:TPU:0, one launch (start us, length us, event | category | flops | bytes accessed | tf_op | source)
XLA Modules:
  0.0 132.5 jit_solution(8606572700474487680)
XLA Ops:
  0.0 0.7 maximum_bitcast_fusion
  0.7 0.7 bitcast_convert_fusion
  1.4 0.7 maximum_convert_fusion
  2.1 1.3 pad_maximum_fusion.wt_ref
  3.4 0.7 copy.18.par_ref
  4.1 0.1 copy.19.bo_ref
  4.2 59.1 %exchange.1 = (bf16[3072,256]{1,0:T(8,128)(2,1)}, bf16[3,32,256,128]{3,2,1,0:T(8,128)(2,1)}, f32[96,384]{1,0:T(8,128)}, bf16[128,1024]{1,0:T(8,128)(2,1)}) custom-call(bf16[32,64,384]{2,1,0:T(8,128)(2,1)} %bitcast.10, s32[32,384]{1,0:T(8,128)} %mask_ref.1, f32[64,3]{1,0:T(8,128)} %copy.18.par_ref, bf16[64,64]{1,0:T(8,128)(2,1)} %pad_maximum_fusion.wt_ref, ...), custom_call_target="tpu_custom_call" | custom-call | tf_op jit(solution)/shard_map/exchange/pallas_call | solution.py:233
  63.4 0.0 copy-start
  63.4 2.8 %copy-done = bf16[3,32,256,128]{3,2,1,0:T(8,128)(2,1)S(1)} copy-done((bf16[3,32,256,128]{3,2,1,0:T(8,128)(2,1)S(1)}, bf16[3,32,256,128]{3,2,1,0:T(8,128)(2,1)}, u32[]{:S(2)}) %copy-start) | copy-done | bytes 6291480
  66.1 0.0 copy-start.1
  66.1 1.4 %copy-done.1 = bf16[3072,256]{1,0:T(8,128)(2,1)S(1)} copy-done((bf16[3072,256]{1,0:T(8,128)(2,1)S(1)}, bf16[3072,256]{1,0:T(8,128)(2,1)}, u32[]{:S(2)}) %copy-start.1) | copy-done | bytes 1572888
  67.6 0.0 copy-start.2
  67.6 0.9 copy-done.2
  68.5 0.0 copy-start.3
  68.5 0.9 copy-done.3
  69.4 63.0 %form.1 = f32[96,384,128]{2,1,0:T(8,128)} custom-call(bf16[3072,256]{1,0:T(8,128)(2,1)S(1)} %copy-done.1, bf16[3,32,256,128]{3,2,1,0:T(8,128)(2,1)S(1)} %copy-done, f32[96,384]{1,0:T(8,128)S(1)} %copy-done.3, bf16[128,1024]{1,0:T(8,128)(2,1)S(1)} %copy-done.2, f32[128,1]{1,0:T(8,128)S(1)} %copy.19.bo_ref, f32[96,384,128]{2,1,0:T(8,128)} %z_ref.1), custom_call_target="tpu_custom_call" | custom-call | tf_op jit(solution)/shard_map/form/pallas_call | solution.py:287
Async XLA Ops:
  63.4 2.8 %copy-start = (bf16[3,32,256,128]{3,2,1,0:T(8,128)(2,1)S(1)}, bf16[3,32,256,128]{3,2,1,0:T(8,128)(2,1)}, u32[]{:S(2)}) copy-start(bf16[3,32,256,128]{3,2,1,0:T(8,128)(2,1)} %get-tuple-element.10.ball_ref) | copy-start | bytes 18874372
  66.1 1.4 %copy-start.1 = (bf16[3072,256]{1,0:T(8,128)(2,1)S(1)}, bf16[3072,256]{1,0:T(8,128)(2,1)}, u32[]{:S(2)}) copy-start(bf16[3072,256]{1,0:T(8,128)(2,1)} %get-tuple-element.9.at_ref) | copy-start | bytes 4718596
  67.6 0.9 copy-start.2
  68.5 0.9 copy-start.3

commit v2 on v1

--- a/solution.py
+++ b/solution.py
@@ -194,7 +194,7 @@
                 atf[half, pl.ds(4 * g + k, ROWS, stride=C), :] = w
     for blk in range(12):
         for half in range(2):
-            at_ref[blk * 256:(blk + 1) * 256, half * 128:(half + 1) * 128] = (
+            at_ref[half, blk * 256:(blk + 1) * 256, :] = (
                 atf[half, blk * 256:(blk + 1) * 256, :].astype(jnp.bfloat16))
 
     got_b(1, 'x')
@@ -233,7 +233,7 @@
     return pl.pallas_call(
         exchange_kernel,
         out_shape=(
-            jax.ShapeDtypeStruct((ROWS * C, S), jnp.bfloat16),
+            jax.ShapeDtypeStruct((2, ROWS * C, 128), jnp.bfloat16),
             jax.ShapeDtypeStruct((JC, C, S, 128), jnp.bfloat16),
             jax.ShapeDtypeStruct((ROWS, N), jnp.float32),
             jax.ShapeDtypeStruct((E, C * C), jnp.bfloat16),
@@ -258,50 +258,86 @@
     )(xt, mask, par, wt, w_out)
 
 
+def first_product(at, rhs_of, hi_ref, lo_ref, slot, p):
+    o = jnp.dot(at, rhs_of(p), preferred_element_type=jnp.float32)
+    hi = o.astype(jnp.bfloat16)
+    lo = (o - hi.astype(jnp.float32)).astype(jnp.bfloat16)
+    for i in range(IB):
+        for k in range(2):
+            rr = slice((2 * p + k) * C, (2 * p + k + 1) * C)
+            hi_ref[slot, i, rr, :] = hi[i * C:(i + 1) * C, k * 128:(k + 1) * 128]
+            lo_ref[slot, i, rr, :] = lo[i * C:(i + 1) * C, k * 128:(k + 1) * 128]
+
+
+def second_product(wot, bo, hi_ref, lo_ref, slot, inv_ref, z_ref, out_ref, q):
+    a, b = 2 * q, 2 * q + 1
+    rt = jnp.dot(wot, jnp.concatenate([hi_ref[slot, a], hi_ref[slot, b]], axis=1),
+                 preferred_element_type=jnp.float32)
+    rt = rt + jnp.dot(wot, jnp.concatenate([lo_ref[slot, a], lo_ref[slot, b]], axis=1),
+                      preferred_element_type=jnp.float32)
+    for k, i in enumerate((a, b)):
+        upd = (rt[:, k * 128:(k + 1) * 128] + bo) * inv_ref[i:i + 1, :]
+        out_ref[i] = z_ref[i] + upd.T
+
+
 def form_kernel(at_ref, ball_ref, inv_ref, wot_ref, bo_ref, z_ref, out_ref, hi_ref, lo_ref):
-    at = at_ref[...]
-    for p in range(C // 2):
-        rhs = jnp.concatenate([ball_ref[0, 2 * p], ball_ref[0, 2 * p + 1]], axis=1)
-        o = jnp.dot(at, rhs, preferred_element_type=jnp.float32)
-        hi = o.astype(jnp.bfloat16)
-        lo = (o - hi.astype(jnp.float32)).astype(jnp.bfloat16)
-        for i in range(IB):
-            for k in range(2):
-                rr = slice((2 * p + k) * C, (2 * p + k + 1) * C)
-                ll = slice(i * 128, (i + 1) * 128)
-                hi_ref[rr, ll] = hi[i * C:(i + 1) * C, k * 128:(k + 1) * 128]
-                lo_ref[rr, ll] = lo[i * C:(i + 1) * C, k * 128:(k + 1) * 128]
-    wot = wot_ref[...]
-    bo = bo_ref[...]
-    for q in range(IB // 2):
-        ll = slice(q * 256, (q + 1) * 256)
-        rt = jnp.dot(wot, hi_ref[:, ll], preferred_element_type=jnp.float32)
-        rt = rt + jnp.dot(wot, lo_ref[:, ll], preferred_element_type=jnp.float32)
-        for k in range(2):
-            i = 2 * q + k
-            upd = (rt[:, k * 128:(k + 1) * 128] + bo) * inv_ref[i:i + 1, :]
-            out_ref[i] = z_ref[i] + upd.T
+    n = pl.program_id(0)
+    last = pl.num_programs(0) - 1
+
+    def rhs_of(p):
+        return jnp.concatenate([ball_ref[0, 2 * p], ball_ref[0, 2 * p + 1]], axis=1)
+
+    def step(slot, do_first, do_second):
+        wot, bo = wot_ref[...], bo_ref[...]
+        for p in range(C // 2):
+            if do_first:
+                at = jnp.concatenate([at_ref[0], at_ref[1]], axis=1)
+                first_product(at, rhs_of, hi_ref, lo_ref, slot, p)
+            if do_second and p % 4 == 1:
+                second_product(wot, bo, hi_ref, lo_ref, 1 - slot, inv_ref, z_ref, out_ref, p // 4)
+
+    for slot in range(2):
+        @pl.when((n > 0) & (n < last) & (lax.rem(n, 2) == slot))
+        def _():
+            step(slot, True, True)
+
+    @pl.when(n == 0)
+    def _():
+        step(0, True, False)
+
+    @pl.when(n == last)
+    def _():
+        step((JC * ROWS // IB) % 2, False, True)
 
 
 def form(at, ball, inv, wot, bo, z):
+    ni = ROWS // IB
+    steps = JC * ni
+
+    def now(n):
+        return jnp.minimum(n, steps - 1)
+
+    def prev(n):
+        return jnp.maximum(n - 1, 0)
+
     return pl.pallas_call(
         form_kernel,
-        grid=(JC, ROWS // IB),
+        grid=(steps + 1,),
         out_shape=jax.ShapeDtypeStruct((ROWS, N, E), jnp.float32),
         in_specs=[
-            pl.BlockSpec((IB * C, S), lambda j, i: (i, 0)),
-            pl.BlockSpec((1, C, S, 128), lambda j, i: (j, 0, 0, 0)),
-            pl.BlockSpec((IB, 128), lambda j, i: (i, j)),
-            pl.BlockSpec((E, C * C), lambda j, i: (0, 0)),
-            pl.BlockSpec((E, 1), lambda j, i: (0, 0)),
-            pl.BlockSpec((IB, 128, E), lambda j, i: (i, j, 0)),
+            pl.BlockSpec((2, IB * C, 128), lambda n: (0, now(n) % ni, 0)),
+            pl.BlockSpec((1, C, S, 128), lambda n: (now(n) // ni, 0, 0, 0)),
+            pl.BlockSpec((IB, 128), lambda n: (prev(n) % ni, prev(n) // ni)),
+            pl.BlockSpec((E, C * C), lambda n: (0, 0)),
+            pl.BlockSpec((E, 1), lambda n: (0, 0)),
+            pl.BlockSpec((IB, 128, E), lambda n: (prev(n) % ni, prev(n) // ni, 0)),
         ],
-        out_specs=pl.BlockSpec((IB, 128, E), lambda j, i: (i, j, 0)),
+        out_specs=pl.BlockSpec((IB, 128, E), lambda n: (prev(n) % ni, prev(n) // ni, 0)),
         scratch_shapes=[
-            pltpu.VMEM((C * C, IB * 128), jnp.bfloat16),
-            pltpu.VMEM((C * C, IB * 128), jnp.bfloat16),
+            pltpu.VMEM((2, IB, C * C, 128), jnp.bfloat16),
+            pltpu.VMEM((2, IB, C * C, 128), jnp.bfloat16),
         ],
-        compiler_params=pltpu.CompilerParams(vmem_limit_bytes=40 * 1024 * 1024),
+        compiler_params=pltpu.CompilerParams(vmem_limit_bytes=60 * 1024 * 1024),
         name='form',
     )(at, ball, inv, wot, bo, z)
 

time: 133 us -> 120 us (0.902)
  Pallas kernels: 122 us -> 115 us
  local copies, waits for them, and re-layouts: 6.86 us -> 1.45 us
    pallas_call x2, Pallas kernels: 122 us -> 115 us  [the longest x1 59.1 us: exchange(): pl.pallas_call(exchange_kernel, out_shape=(jax.ShapeDtypeStruct((2, ROWS...]
    unnamed x8 -> x0, local copies, waits for them, and re-layouts: 6.04 us -> none
where the time goes in v2:
time: 120 us
  Pallas kernels  115 us (96%)
  other arithmetic  3.4 us (3%)
  local copies, waits for them, and re-layouts  1.45 us (1%)
    pallas_call x1, Pallas kernels, exchange(): pl.pallas_call(exchange_kernel, out_shape=(jax.ShapeDtypeStruct((2, ROWS...  59.1 us
    pallas_call x1, Pallas kernels, form(): pl.pallas_call(form_kernel, grid=(steps + 1,), out_shape=jax.ShapeDtypeSt...  55.7 us

profile of v2, /device:TPU:0, one launch (start us, length us, event | category | flops | bytes accessed | tf_op | source)
XLA Modules:
  0.0 119.7 jit_solution(16820843237842695276)
XLA Ops:
  0.0 0.7 maximum_bitcast_fusion
  0.7 0.7 bitcast_convert_fusion
  1.4 0.7 maximum_convert_fusion
  2.1 1.3 %pad_maximum_fusion.wt_ref = bf16[64,64]{1,0:T(8,128)(2,1)} fusion(bf16[32,64]{1,0:T(8,128)(2,1)} %bitcast.11, bf16[32,64]{1,0:T(8,128)(2,1)} %bitcast.12), kind=kLoop, calls=%fused_computation | loop fusion | flops 16384 | bytes 16384 | tf_op jit(solution)/shard_map/concatenate | solution.py:352
  3.4 0.7 copy.18.par_ref
  4.1 0.7 copy.19.bo_ref
  4.9 59.1 %exchange.1 = (bf16[2,3072,128]{2,1,0:T(8,128)(2,1)}, bf16[3,32,256,128]{3,2,1,0:T(8,128)(2,1)}, f32[96,384]{1,0:T(8,128)}, bf16[128,1024]{1,0:T(8,128)(2,1)}) custom-call(bf16[32,64,384]{2,1,0:T(8,128)(2,1)} %bitcast.10, s32[32,384]{1,0:T(8,128)} %mask_ref.1, f32[64,3]{1,0:T(8,128)} %copy.18.par_ref, bf16[64,64]{1,0:T(8,128)(2,1)} %pad_maximum_fusion.wt_ref, ...), custom_call_target="tpu_custom_call" | custom-call | tf_op jit(solution)/shard_map/exchange/pallas_call | solution.py:233
  64.0 55.7 %form.1 = f32[96,384,128]{2,1,0:T(8,128)} custom-call(bf16[2,3072,128]{2,1,0:T(8,128)(2,1)} %get-tuple-element.9.at_ref, bf16[3,32,256,128]{3,2,1,0:T(8,128)(2,1)} %get-tuple-element.10.ball_ref, f32[96,384]{1,0:T(8,128)} %get-tuple-element.11.inv_ref, bf16[128,1024]{1,0:T(8,128)(2,1)} %get-tuple-element.12.wot_ref, f32[128,1]{1,0:T(8,128)} %copy.19.bo_ref, ...), custom_call_target="tpu_custom_call" | custom-call | tf_op jit(solution)/shard_map/form/pallas_call | solution.py:323

commit v3 on v0

v3 whole, which is shorter than its diff:
```python
import jax
import jax.numpy as jnp
from jax import lax
from jax.experimental import pallas as pl
from jax.experimental.pallas import tpu as pltpu
from jax.sharding import PartitionSpec as P

MESH = pl.DeviceIdType.MESH
L = 128
S_LOC, N, K, C, E = 32, 384, 64, 32, L
S = 256
ROWS = 96
HALF = 48
JC = 3
CG = 8
D_VIA_X = (24, 24, 24)
IB = 8
EARLY = 18
CHUNKS = JC * ROWS // IB
VMEM_LIMIT = 65011712
F32, BF16 = jnp.float32, jnp.bfloat16


def first_product(at_ref, row0, ball_ref, t, hi_ref, lo_ref, slot, p):
    at = jnp.concatenate([at_ref[0, pl.ds(row0, IB * C), :], at_ref[1, pl.ds(row0, IB * C), :]], axis=1)
    rhs = jnp.concatenate([ball_ref[t, 2 * p], ball_ref[t, 2 * p + 1]], axis=1)
    o = jnp.dot(at, rhs, preferred_element_type=F32)
    hi = o.astype(BF16)
    lo = (o - hi.astype(F32)).astype(BF16)
    for i in range(IB):
        for k in range(2):
            rr = slice((2 * p + k) * C, (2 * p + k + 1) * C)
            hi_ref[slot, i, rr, :] = hi[i * C:(i + 1) * C, k * L:(k + 1) * L]
            lo_ref[slot, i, rr, :] = lo[i * C:(i + 1) * C, k * L:(k + 1) * L]


def second_product(wot, bo, hi_ref, lo_ref, slot, inv, z_ref, out_ref, buf, q):
    a, b = 2 * q, 2 * q + 1
    rt = jnp.dot(wot, jnp.concatenate([hi_ref[slot, a], hi_ref[slot, b]], axis=1),
                 preferred_element_type=F32)
    rt = rt + jnp.dot(wot, jnp.concatenate([lo_ref[slot, a], lo_ref[slot, b]], axis=1),
                      preferred_element_type=F32)
    for k, i in enumerate((a, b)):
        upd = (rt[:, k * L:(k + 1) * L] + bo) * inv[i:i + 1, :]
        out_ref[buf[0], buf[1], i] = z_ref[buf[0], buf[1], i] + upd.T


def form_chunks(k0, k1, at_ref, ball_ref, t_base, inv_ref, wot_ref, bo_ref, z_hbm, dst_of,
                hi_ref, lo_ref, zbuf, obuf, zsem, osem, event):
    m0, m1 = k0 // 2, k1 // 2

    def z_copy(k, st, pos):
        i0 = pl.multiple_of(lax.rem(k, 12) * IB, IB)
        j0 = pl.multiple_of((k // 12) * L, L)
        return pltpu.make_async_copy(z_hbm.at[pl.ds(i0, IB), pl.ds(j0, L), :], zbuf.at[st, pos], zsem.at[st, pos])

    def o_copy(k, st, pos):
        return pltpu.make_async_copy(obuf.at[st, pos], dst_of(k), osem.at[st, pos])

    z_copy(k0, lax.rem(m0, 2), 1).start()

    def inv_of(k):
        i0 = pl.multiple_of(lax.rem(k, 12) * IB, IB)
        return inv_ref[k // 12, pl.ds(i0, IB), :]

    def body(m, carry):
        st = lax.rem(m, 2)
        event(m)
        z_copy(2 * m + 1, 1 - st, 0).start()

        @pl.when(m < m1 - 1)
        def _():
            z_copy(2 * m + 2, 1 - st, 1).start()

        @pl.when(m > m0)
        def _():
            z_copy(2 * m - 1, st, 0).wait()

        z_copy(2 * m, st, 1).wait()

        @pl.when(m > m0 + 2)
        def _():
            o_copy(2 * m - 5, st, 0).wait()

        @pl.when(m > m0 + 1)
        def _():
            o_copy(2 * m - 4, st, 1).wait()

        t = m // 6 - t_base
        wot, bo = wot_ref[...], bo_ref[...]
        for slot in range(2):
            k = 2 * m + slot
            row0 = pl.multiple_of(lax.rem(k, 12) * (IB * C), IB * C)
            prev = jnp.maximum(k - 1, k0)
            inv = inv_of(prev)
            for p in range(C // 2):
                first_product(at_ref, row0, ball_ref, t, hi_ref, lo_ref, slot, p)
                if p % 4 == 1:
                    second_product(wot, bo, hi_ref, lo_ref, 1 - slot, inv, zbuf, obuf, (st, slot), p // 4)

        @pl.when(m > m0)
        def _():
            o_copy(2 * m - 1, st, 0).start()

        o_copy(2 * m, st, 1).start()
        return carry

    lax.fori_loop(m0, m1, body, 0)

    st = m1 % 2
    z_copy(k1 - 1, st, 0).wait()
    if m1 - m0 > 2:
        o_copy(2 * m1 - 5, st, 0).wait()
    wot, bo, inv = wot_ref[...], bo_ref[...], inv_of(k1 - 1)
    for q in range(IB // 2):
        second_product(wot, bo, hi_ref, lo_ref, 1, inv, zbuf, obuf, (st, 0), q)
    o_copy(k1 - 1, st, 0).start()
    return [o_copy(2 * m1 - 4, m1 % 2, 1), o_copy(2 * m1 - 3, 1 - st, 0),
            o_copy(2 * m1 - 2, 1 - st, 1), o_copy(k1 - 1, st, 0)]


def exchange_kernel(x_ref, mask_ref, ga_ref, be_ref, wa_ref, ba_ref, wb_ref, bb_ref, wo_ref, bo_in, z_hbm,
                    inv_ref, wot_ref, bo_ref, at_out, b_out, p_out,
                    row_s, keep_s, stage, ta, ra, rp, mall, atf, at_ref, ball_ref, wof, ns,
                    hi_ref, lo_ref, zbuf, obuf, ssem, rsem, zsem, osem, lsem):
    y = lax.axis_index('seq')
    r = lax.axis_index('dap')
    x = r // 2
    c = r % 2
    me = y * 4 + r
    dev_x = (0, y, (1 - x) * 2 + c)
    dev_y = (0, 1 - y, r)
    dev_p = (0, y, x * 2 + 1 - c)
    id_x = y * 4 + (1 - x) * 2 + c
    id_y = (1 - y) * 4 + r
    id_xy = (1 - y) * 4 + (1 - x) * 2 + c
    id_p = y * 4 + x * 2 + 1 - c
    id_px = y * 4 + (1 - x) * 2 + 1 - c
    id_py = (1 - y) * 4 + x * 2 + 1 - c
    id_pd = (1 - y) * 4 + (1 - x) * 2 + 1 - c

    barrier = pltpu.get_barrier_semaphore()
    flips = [(fy, fr) for fy in range(2) for fr in range(4) if fy or fr]
    for fy, fr in flips:
        peer = (0, (y + fy) % 2, (r + fr) % 4)
        pl.semaphore_signal(barrier, inc=1, device_id=peer, device_id_type=MESH)

    def rows_of(dev_id):
        return pl.ds(pl.multiple_of(dev_id * S_LOC, S_LOC), S_LOC)

    my_rows = rows_of(me)
    sends = []

    def copy(src, dst, k, dev):
        return pltpu.make_async_remote_copy(
            src_ref=src, dst_ref=dst, send_sem=ssem.at[k], recv_sem=rsem.at[k],
            device_id=dev, device_id_type=MESH)

    def send(refs, k, dev):
        copy(*refs(), k, dev).start()
        sends.append(lambda: copy(*refs(), k, dev).wait_send())

    def arrived(ref, k):
        copy(ref, ref, k, dev_p).wait_recv()

    def b_part(t, dev_id, lo=0, hi=C):
        return ball_ref.at[t, pl.ds(lo, hi - lo), rows_of(dev_id), :]

    def ak(h, what):
        return h * 7 + ['x', 'y', 'd', 'po', 'px', 'py', 'pd'].index(what)

    M0 = 14

    def bk(t, what):
        return 21 + t * 9 + ['x', 'y', 'dx', 'dy', 'po', 'px', 'py', 'pdx', 'pdy'].index(what)

    def send_b(t, *to):
        for w in to:
            dev = {'x': dev_x, 'y': dev_y, 'po': dev_p}[w]
            send(lambda: (b_part(t, me),) * 2, bk(t, w), dev)

    def got_b(t, *frm):
        v = D_VIA_X[t]
        for w in frm:
            if w == 'x':
                arrived(b_part(t, id_x), bk(t, 'x'))
                send(lambda: (b_part(t, id_x, v, C),) * 2, bk(t, 'dy'), dev_y)
                send(lambda: (b_part(t, id_x),) * 2, bk(t, 'px'), dev_p)
            elif w == 'y':
                arrived(b_part(t, id_y), bk(t, 'y'))
                send(lambda: (b_part(t, id_y, 0, v),) * 2, bk(t, 'dx'), dev_x)
                send(lambda: (b_part(t, id_y),) * 2, bk(t, 'py'), dev_p)
            elif w == 'dx':
                arrived(b_part(t, id_xy, 0, v), bk(t, 'dx'))
                send(lambda: (b_part(t, id_xy, 0, v),) * 2, bk(t, 'pdx'), dev_p)
            else:
                arrived(b_part(t, id_xy, v, C), bk(t, 'dy'))
                send(lambda: (b_part(t, id_xy, v, C),) * 2, bk(t, 'pdy'), dev_p)

    def got_b_partner(t):
        v = D_VIA_X[t]
        arrived(b_part(t, id_p), bk(t, 'po'))
        arrived(b_part(t, id_px), bk(t, 'px'))
        arrived(b_part(t, id_py), bk(t, 'py'))
        arrived(b_part(t, id_pd, 0, v), bk(t, 'pdx'))
        arrived(b_part(t, id_pd, v, C), bk(t, 'pdy'))

    own, other = 2 * x, 2 * (1 - x)

    def got_a(h, w):
        n = 'xyd'.index(w)
        arrived(ra.at[n, h], ak(h, w))
        if w == 'x':
            send(lambda: (ra.at[0, h], ra.at[2, h]), ak(h, 'd'), dev_y)
        send(lambda: (ra.at[n, h, 1 - c], rp.at[n + 1, h]), ak(h, 'p' + w), dev_p)

    row_s[0:1, 0:64] = ga_ref[...].astype(F32)
    row_s[0:1, 64:L] = be_ref[...].astype(F32)
    row_s[1:2, 0:32] = ba_ref[...].astype(F32)
    row_s[1:2, 32:64] = bb_ref[...].astype(F32)
    row_s[1:2, 64:L] = jnp.zeros((1, 64), F32)
    cols = jnp.broadcast_to(row_s[0:1, :], (L, L)).T
    gamma, beta = cols[0:64, :], cols[64:L, :]
    bias = jnp.broadcast_to(row_s[1:2, :], (L, L)).T[0:64, :]
    wt = jnp.concatenate([wa_ref[...], wb_ref[...]], axis=0)
    mall[my_rows, :] = mask_ref[...].astype(F32).astype(BF16)
    for t in range(JC):
        keep_s[t] = mask_ref[:, t * L:(t + 1) * L].astype(F32)

    def project(t):
        ll = slice(t * L, (t + 1) * L)

        def two_seqs(s2, carry):
            xs = []
            for u in range(2):
                v = x_ref[2 * s2 + u, :, ll].astype(F32)
                mean = jnp.sum(v, axis=0, keepdims=True) * (1.0 / K)
                cen = v - mean
                var = jnp.sum(cen * cen, axis=0, keepdims=True) * (1.0 / K)
                xs.append((cen * lax.rsqrt(var + 1e-5) * gamma + beta).astype(BF16))
            out = jnp.dot(wt, jnp.concatenate(xs, axis=1), preferred_element_type=F32)
            for u in range(2):
                keep = keep_s[t, pl.ds(2 * s2 + u, 1), :]
                stage[t, pl.ds(2 * s2 + u, 2 * C, stride=S_LOC), :] = (out[:, u * L:(u + 1) * L] + bias) * keep
            return carry

        lax.fori_loop(0, S_LOC // 2, two_seqs, 0, unroll=4)
        for d in range(C):
            ball_ref[t, d, my_rows, :] = stage[t, (C + d) * S_LOC:(C + d + 1) * S_LOC, :].astype(BF16)
        for g in range(CG):
            blk = stage[t, g * L:(g + 1) * L, :].T.astype(BF16)
            lo = t * L
            while lo < (t + 1) * L:
                q = lo // HALF
                hi = min((q + 1) * HALF, (t + 1) * L)
                ta[q // 2, q % 2, g, lo - q * HALF:hi - q * HALF, :] = blk[lo - t * L:hi - t * L, :]
                lo = hi

    project(0)
    pl.semaphore_wait(barrier, 7)
    send_b(0, 'x', 'y', 'po')
    for n, (fy, fr) in enumerate(flips):
        peer = (0, (y + fy) % 2, (r + fr) % 4)
        send(lambda: (mall.at[my_rows],) * 2, M0 + n, peer)
    project(1)
    project(2)
    for h in range(2):
        send(lambda h=h: (ta.at[own + 1 - c, h], rp.at[0, h]), ak(h, 'po'), dev_p)
    send(lambda: (ta.at[pl.ds(other, 2), 0], ra.at[0, 0]), ak(0, 'x'), dev_x)
    send(lambda: (ta.at[pl.ds(own, 2), 0], ra.at[1, 0]), ak(0, 'y'), dev_y)

    wof[...] = wo_ref[...].astype(F32)
    for g in range(CG):
        parts = [wof[pl.ds(4 * g + k, C, stride=C), :] for k in range(4)]
        wot_ref[:, g * L:(g + 1) * L] = jnp.concatenate(parts, axis=0).T.astype(BF16)
    bo_ref[...] = jnp.broadcast_to(bo_in[...].astype(F32), (E, E)).T

    got_b(0, 'x', 'y')
    send(lambda: (ta.at[pl.ds(other, 2), 1], ra.at[0, 1]), ak(1, 'x'), dev_x)

    for n, (fy, fr) in enumerate(flips):
        frm = ((y - fy + 2) % 2) * 4 + (r - fr + 4) % 4
        arrived(mall.at[rows_of(frm)], M0 + n)
    mm = mall[...]
    ns[...] = lax.dot_general(mm, mm, (((0,), (0,)), ((), ())), preferred_element_type=F32)
    for t in range(JC):
        inv_ref[t] = 1.0 / (1e-3 + ns[pl.ds(pl.multiple_of(r * ROWS, 32), ROWS), t * L:(t + 1) * L])

    got_a(0, 'x')
    send(lambda: (ta.at[pl.ds(own, 2), 1], ra.at[1, 1]), ak(1, 'y'), dev_y)
    send_b(1, 'x', 'po')
    got_a(0, 'y')
    got_b(0, 'dy', 'dx')
    got_a(0, 'd')

    lane = lax.broadcasted_iota(jnp.int32, (HALF, L), 1)
    low = lane < 64
    odd = lax.rem(lane // 32, 2) == 1

    def left_operand(h):
        for n in range(4):
            arrived(rp.at[n, h], ak(h, 'p' + 'oxyd'[n]))
        for half in range(2):
            for g in range(CG):
                v = []
                for q in range(4):
                    sx, sc = q // 2, q % 2
                    slot = (sx != x).astype(jnp.int32) + 2 * (half != y).astype(jnp.int32)
                    own_v = ta[r, h, g].astype(F32)
                    far_v = ra[jnp.maximum(slot - 1, 0), h, c, g].astype(F32)
                    in_plane = jnp.where(slot == 0, own_v, far_v)
                    v.append(jnp.where(sc == c, in_plane, rp[slot, h, g].astype(F32)))
                r0, r1, r2, r3 = [pltpu.roll(u, 64, 1) for u in v]
                n0 = jnp.where(low, v[0], r2)
                n1 = jnp.where(low, v[1], r3)
                n2 = jnp.where(low, r0, v[2])
                n3 = jnp.where(low, r1, v[3])
                w0 = jnp.where(odd, pltpu.roll(n1, 32, 1), n0)
                w1 = jnp.where(odd, n1, pltpu.roll(n0, 96, 1))
                w2 = jnp.where(odd, pltpu.roll(n3, 32, 1), n2)
                w3 = jnp.where(odd, n3, pltpu.roll(n2, 96, 1))
                for k, w in enumerate((w0, w1, w2, w3)):
                    atf[half, pl.ds(4 * g + k, HALF, stride=C), :] = w
        hc = HALF * C
        for half in range(2):
            for blk in range(6):
                at_ref[half, h * hc + blk * 256:h * hc + (blk + 1) * 256, :] = (
                    atf[half, blk * 256:(blk + 1) * 256, :].astype(BF16))

    left_operand(0)
    got_b_partner(0)

    at_copy = pltpu.make_async_copy(at_ref, at_out, lsem.at[0])
    b_copy = [pltpu.make_async_copy(ball_ref.at[t], b_out.at[t - 1], lsem.at[t]) for t in (1, 2)]

    def event(m):
        @pl.when(m == 1)
        def _():
            got_a(1, 'x')
            send_b(1, 'y')
            send_b(2, 'x', 'po')
            got_a(1, 'y')

        @pl.when(m == 3)
        def _():
            got_b(1, 'x')
            send_b(2, 'y')
            got_a(1, 'd')
            left_operand(1)
            at_copy.start()

        @pl.when(m == 5)
        def _():
            got_b(1, 'y')
            got_b(2, 'x')

        @pl.when(m == 6)
        def _():
            got_b(1, 'dx', 'dy')
            got_b_partner(1)
            b_copy[0].start()

        @pl.when(m == 7)
        def _():
            got_b(2, 'y')

        @pl.when(m == 8)
        def _():
            got_b(2, 'dy')

    outs = form_chunks(0, EARLY, at_ref, ball_ref, 0, inv_ref, wot_ref, bo_ref, z_hbm,
                       lambda k: p_out.at[pl.ds(pl.multiple_of(k * IB, IB), IB)],
                       hi_ref, lo_ref, zbuf, obuf, zsem, osem, event)
    got_b(2, 'dx')
    got_b_partner(2)
    b_copy[1].start()
    for sent in sends:
        sent()
    for cp in outs:
        cp.wait()
    at_copy.wait()
    for cp in b_copy:
        cp.wait()


def exchange(xt, mask, ga, be, wa, ba, wb, bb, w_out, bo, z):
    vm = pl.BlockSpec(memory_space=pltpu.VMEM)
    hbm = pl.BlockSpec(memory_space=pl.ANY)
    nsem = 21 + 9 * JC
    return pl.pallas_call(
        exchange_kernel,
        out_shape=(
            jax.ShapeDtypeStruct((JC, ROWS, L), F32),
            jax.ShapeDtypeStruct((E, C * C), BF16),
            jax.ShapeDtypeStruct((E, E), F32),
            jax.ShapeDtypeStruct((2, ROWS * C, L), BF16),
            jax.ShapeDtypeStruct((2, C, S, L), BF16),
            jax.ShapeDtypeStruct((EARLY * IB, L, E), F32),
        ),
        in_specs=[vm] * 10 + [hbm],
        out_specs=(vm,) * 3 + (hbm,) * 3,
        scratch_shapes=[
            pltpu.VMEM((8, L), F32),
            pltpu.VMEM((JC, S_LOC, L), F32),
            pltpu.VMEM((JC, 2 * C * S_LOC, L), F32),
            pltpu.VMEM((4, 2, CG, HALF, L), BF16),
            pltpu.VMEM((3, 2, 2, CG, HALF, L), BF16),
            pltpu.VMEM((4, 2, CG, HALF, L), BF16),
            pltpu.VMEM((S, N), BF16),
            pltpu.VMEM((2, HALF * C, L), F32),
            pltpu.VMEM((2, ROWS * C, L), BF16),
            pltpu.VMEM((JC, C, S, L), BF16),
            pltpu.VMEM((C * C, E), F32),
            pltpu.VMEM((N, N), F32),
            pltpu.VMEM((2, IB, C * C, L), BF16),
            pltpu.VMEM((2, IB, C * C, L), BF16),
            pltpu.VMEM((2, 2, IB, L, E), F32),
            pltpu.VMEM((2, 2, IB, L, E), F32),
            pltpu.SemaphoreType.DMA((nsem,)),
            pltpu.SemaphoreType.DMA((nsem,)),
            pltpu.SemaphoreType.DMA((2, 2)),
            pltpu.SemaphoreType.DMA((2, 2)),
            pltpu.SemaphoreType.DMA((3,)),
        ],
        compiler_params=pltpu.CompilerParams(
            collective_id=0, has_side_effects=True, vmem_limit_bytes=VMEM_LIMIT),
        name='exchange',
    )(xt, mask, ga, be, wa, ba, wb, bb, w_out, bo, z)


def form_kernel(inv_ref, wot_ref, bo_ref, at_hbm, b_hbm, p_hbm, z_hbm, out_hbm,
                at_ref, ball_ref, pbuf, hi_ref, lo_ref, zbuf, obuf, zsem, osem, lsem, psem):
    at_copy = pltpu.make_async_copy(at_hbm, at_ref, lsem.at[0])
    b_copy = [pltpu.make_async_copy(b_hbm.at[t], ball_ref.at[t], lsem.at[1 + t]) for t in range(2)]
    at_copy.start()
    b_copy[0].start()
    b_copy[1].start()

    units = EARLY // 6
    u_rows = 6 * IB
    p_in = [pltpu.make_async_copy(p_hbm.at[pl.ds(u * u_rows, u_rows)], pbuf.at[u], psem.at[0, u])
            for u in range(units)]
    p_out = [pltpu.make_async_copy(
        pbuf.at[u], out_hbm.at[pl.ds((u % 2) * u_rows, u_rows), pl.ds((u // 2) * L, L), :], psem.at[1, u])
        for u in range(units)]

    def dst_of(k):
        i0 = pl.multiple_of(lax.rem(k, 12) * IB, IB)
        j0 = pl.multiple_of((k // 12) * L, L)
        return out_hbm.at[pl.ds(i0, IB), pl.ds(j0, L), :]

    m0 = EARLY // 2

    def event(m):
        for u in range(units):
            @pl.when(m == m0 + 1 + u)
            def _():
                p_in[u].start()

            @pl.when(m == m0 + 3 + u)
            def _():
                p_in[u].wait()
                p_out[u].start()

        @pl.when(m == m0 + 3)
        def _():
            b_copy[1].wait()

    at_copy.wait()
    b_copy[0].wait()
    outs = form_chunks(EARLY, CHUNKS, at_ref, ball_ref, 1, inv_ref, wot_ref, bo_ref, z_hbm, dst_of,
                       hi_ref, lo_ref, zbuf, obuf, zsem, osem, event)
    for cp in outs + p_out:
        cp.wait()


def form(inv, wot, bo, at, ball, part, z):
    vm = pl.BlockSpec(memory_space=pltpu.VMEM)
    hbm = pl.BlockSpec(memory_space=pl.ANY)
    return pl.pallas_call(
        form_kernel,
        out_shape=jax.ShapeDtypeStruct((ROWS, N, E), F32),
        in_specs=[vm] * 3 + [hbm] * 4,
        out_specs=hbm,
        scratch_shapes=[
            pltpu.VMEM((2, ROWS * C, L), BF16),
            pltpu.VMEM((2, C, S, L), BF16),
            pltpu.VMEM((EARLY // 6, 6 * IB, L, E), F32),
            pltpu.VMEM((2, IB, C * C, L), BF16),
            pltpu.VMEM((2, IB, C * C, L), BF16),
            pltpu.VMEM((2, 2, IB, L, E), F32),
            pltpu.VMEM((2, 2, IB, L, E), F32),
            pltpu.SemaphoreType.DMA((2, 2)),
            pltpu.SemaphoreType.DMA((2, 2)),
            pltpu.SemaphoreType.DMA((3,)),
            pltpu.SemaphoreType.DMA((2, EARLY // 6)),
        ],
        compiler_params=pltpu.CompilerParams(vmem_limit_bytes=VMEM_LIMIT),
        name='form',
    )(inv, wot, bo, at, ball, part, z)


def solution(mesh):
    rows = P(('data', 'seq', 'dap'), None, None)
    mask_spec = P(('data', 'seq', 'dap'), None)
    pair_spec = P(('data', 'dap'), None, None)

    def device_step(msa, mask, pair, ln_gamma, ln_beta, w_a, b_a, w_b, b_b, w_out, b_out):
        inv, wot, bo, at, ball, part = exchange(
            jnp.swapaxes(msa, 1, 2), mask, ln_gamma[None], ln_beta[None], w_a.T, b_a[None], w_b.T, b_b[None],
            w_out, b_out[None], pair)
        return form(inv, wot, bo, at, ball, part, pair)

    return jax.shard_map(device_step, mesh=mesh, in_specs=(rows, mask_spec, pair_spec) + (P(),) * 8,
                         out_specs=pair_spec, check_vma=False)
```

time: 609 us -> 99.1 us (0.16)
  waiting for transfers between devices: 488 us -> 0 us
  Pallas kernels: 0 us -> 99 us
  matrix products: 73.7 us -> 0 us
  other arithmetic: 26.9 us -> 0 us
  between operations: 13.3 us -> 0.01 us
  local copies, waits for them, and re-layouts: 6.22 us -> 0 us
    reduce_scatter x2 -> x0, waiting for transfers between devices: 253 us -> none  [the longest x1 253 us: device_step(): rows_r = lax.psum_scatter(part_r, 'dap', scatter_dimension=0, tiled=True)]
    psum x2 -> x0, waiting for transfers between devices: 234 us -> none  [the longest x1 216 us: device_step(): rows_r = lax.psum(rows_r, 'seq')]
    pallas_call x0 -> x2, Pallas kernels: none -> 99 us  [the longest x1 68.9 us: exchange(): pl.pallas_call(exchange_kernel, out_shape=(jax.ShapeDtypeStruct((JC, ROWS...]
    dot_general x4 -> x0, matrix products: 73.7 us -> none  [the longest x1 71 us: device_step(): jnp.einsum('side,sjd->ije', lifted, right, preferred_element_type=jnp.flo...]
    add x2 -> x0, other arithmetic: 21.1 us -> none  [the longest x1 20.2 us: device_step(): return pair_local + update]
  transfers between devices with their start and end apart: 4 -> 0, of which waited for: 3 -> 0; matrix products, arithmetic and copies ran while one was open for 14% -> 0% of each run, Pallas kernels for 0% -> 0%
where the time goes in v3:
time: 99.1 us; the launch traced here: 99 us
  Pallas kernels  99 us (100%)
    pallas_call x1, Pallas kernels, exchange(): pl.pallas_call(exchange_kernel, out_shape=(jax.ShapeDtypeStruct((JC, ROWS...  68.9 us
    pallas_call x1, Pallas kernels, form(): pl.pallas_call(form_kernel, out_shape=jax.ShapeDtypeStruct((ROWS, N, E),...  30.1 us

profile of v3, /device:TPU:0, one launch (start us, length us, event | category | flops | bytes accessed | tf_op | source)
XLA Modules:
  0.0 99.0 jit_solution(15538722153853894416)
XLA Ops:
  0.0 68.9 %exchange.1 = (f32[3,96,128]{2,1,0:T(8,128)}, bf16[128,1024]{1,0:T(8,128)(2,1)}, f32[128,128]{1,0:T(8,128)}, bf16[2,3072,128]{2,1,0:T(8,128)(2,1)}, bf16[2,32,25...) custom-call(bf16[32,64,384]{2,1,0:T(8,128)(2,1)} %bitcast.8, s32[32,384]{1,0:T(8,128)} %mask_ref.1, ...), custom_call_target="tpu_custom_call" | custom-call | tf_op jit(solution)/shard_map/exchange/pallas_call | solution.py:390
  68.9 30.1 %form.1 = f32[96,384,128]{2,1,0:T(8,128)} custom-call(f32[3,96,128]{2,1,0:T(8,128)} %get-tuple-element.11.inv_ref, bf16[128,1024]{1,0:T(8,128)(2,1)} %get-tuple-element.12.wot_ref, f32[128,128]{1,0:T(8,128)} %get-tuple-element.13.bo_ref, bf16[2,3072,128]{2,1,0:T(8,128)(2,1)} %get-tuple-element.14.at_hbm, bf16[2,32,256,128]{3,2,1,0:T(8,128)(2,1)} %get-tuple-element.15.b_hbm, ...), custom_call_target="tpu_custom_call" | custom-call | tf_op jit(solution)/shard_map/form/pallas_call | solution.py:480
